TPU v7x, 128 devices: a whole 4x4x4 slice. The times are simulated.
128 devices in a mesh: trade: 16 (over z, x), path: 8 (over y, core).
Axes of the slice: x: 4, y: 4, z: 4, core: 2. Of those that a mesh axis runs over, the one named last changes fastest.
Arguments:
- coefficients: bfloat16 [32768, 256], P('trade'), may hold values from -6 to 6
- path_basis: bfloat16 [256, 4096], P(None, 'path'), may hold values from -6 to 6
- trade_owner: int32 [32768, 1], P('trade'), may hold values from 0 to 15; in each aligned block of 2048 rows (0 to 2047, 2048 to 4095, ...) at most 192 rows name the same one
- trade_slot: int32 [32768], P('trade'), may hold values from 0 to 63
- set_factor: int32 [1024], P('trade'), may hold values from 0 to 511
- set_level: int32 [1024], P('trade'), may hold values from 0 to 3
- default_date: int32 [512, 4096], P(None, 'path'), may hold values from 0 to 4
- discount: float32 [4], replicated, may hold values from 0.5 to 1
Outputs:
- alloc: float32 [32768], P('trade')
- set_cva: float32 [1024], P('trade')
Inputs may be any that keep to these rules, and one draw needn't show every extreme that they name: `trade_owner`: in the rows of one device no value is named by more than 192 rows, a bound that some block reaches.
All inputs are finite; a program needn't handle non-finite values.
Results may differ from a plain program's by a relative error of at most 0.0045.
Values may be sent and summed in bfloat16 or wider, within the bound.
A program may use at most 64 MiB of HBM per device.

v0:
```python
import jax
import jax.numpy as jnp
from jax import lax
from jax.sharding import PartitionSpec as P

K = 64
DATES = 4


level_step = 1.5


def copy_for_each(shard, axis):
    copies = jnp.broadcast_to(shard, (lax.axis_size(axis), *shard.shape))
    return lax.all_to_all(copies, axis, split_axis=0, concat_axis=0, tiled=True)


def of_everyone(shard, axis):
    return copy_for_each(shard, axis).sum(axis=0)


def in_one(arrays, axis):
    flat, at, gathered = (jnp.concatenate([a.reshape(-1) for a in arrays]), 0, [])
    total = of_everyone(flat, axis)
    for a in arrays:
        gathered.append(total[at : at + a.size].reshape(a.shape))
        at += a.size
    return tuple(gathered)


def trade_values(coefficients, path_basis):
    blocks = []
    for moment in range(DATES):
        blocks.append(
            jnp.dot(
                coefficients[:, moment * K : (moment + 1) * K],
                path_basis[moment * K : (moment + 1) * K, :],
                preferred_element_type=jnp.float32,
            ).astype(jnp.bfloat16)
        )
    return jnp.concatenate(blocks, axis=1)


def owner_weights(netted, set_factor, set_level, default_date, discount):
    per_path = default_date.shape[1]
    paths_total = per_path * lax.axis_size("path")
    factor_rows = (
        set_factor[:, None] == jnp.arange(default_date.shape[0], dtype=jnp.int32)[None, :]
    ).astype(jnp.bfloat16)
    threshold = level_step * set_level.astype(jnp.float32)
    cva_part = jnp.zeros((netted.shape[0],), jnp.float32)
    slope_blocks = []
    for moment in range(DATES):
        struck = (default_date == moment).astype(jnp.bfloat16)
        defaulted = jnp.dot(factor_rows, struck, preferred_element_type=jnp.float32)
        excess = netted[:, moment * per_path : (moment + 1) * per_path] - threshold[:, None]
        weight = defaulted * (discount[moment] / paths_total)
        cva_part = cva_part + jnp.sum(weight * jax.nn.softplus(excess), axis=1)
        slope_blocks.append((weight * jax.nn.sigmoid(excess)).astype(jnp.bfloat16))
    return (cva_part, jnp.concatenate(slope_blocks, axis=1))


def pack_rows(rows, trade_owner, trade_slot):
    owners = lax.axis_size("trade")
    capacity = 3 * rows.shape[0] // (2 * owners)
    owner_cols = (trade_owner == jnp.arange(owners, dtype=jnp.int32)[None, :]).astype(jnp.int32)
    position = jnp.sum(jnp.cumsum(owner_cols, axis=0) * owner_cols, axis=1) - 1
    target_row = trade_owner[:, 0] * capacity + position
    packed = jnp.zeros((owners * capacity, rows.shape[1]), jnp.bfloat16).at[target_row].set(rows)
    labels = (
        jnp.full((owners * capacity,), -1.0, jnp.bfloat16)
        .at[target_row]
        .set(trade_slot.astype(jnp.bfloat16))
    )
    return (
        packed.reshape(owners, capacity, rows.shape[1]),
        labels.reshape(owners, capacity),
        target_row,
    )


def owner_shares(received_rows, arrived_labels, set_factor, set_level, default_date, discount):
    per_path = default_date.shape[1]
    set_local = set_factor.shape[0]
    member = (
        jnp.arange(set_local, dtype=jnp.float32)[:, None]
        == arrived_labels.reshape(-1).astype(jnp.float32)[None, :]
    ).astype(jnp.bfloat16)
    netted = jnp.dot(member, received_rows, preferred_element_type=jnp.float32)
    cva_part, slopes = owner_weights(netted, set_factor, set_level, default_date, discount)
    shares = jnp.zeros((received_rows.shape[0],), jnp.float32)
    for moment in range(DATES):
        looked = lax.dot_general(
            member,
            slopes[:, moment * per_path : (moment + 1) * per_path],
            (((0,), (0,)), ((), ())),
            preferred_element_type=jnp.float32,
        )
        shares = shares + jnp.sum(
            looked
            * received_rows[:, moment * per_path : (moment + 1) * per_path].astype(jnp.float32),
            axis=1,
        )
    return (cva_part, shares)


def on_device(
    coefficients, path_basis, trade_owner, trade_slot, set_factor, set_level, default_date, discount
):
    owners = lax.axis_size("trade")
    packed, labels, target_row = pack_rows(coefficients, trade_owner, trade_slot)
    arrived, arrived_labels = (
        lax.all_to_all(packed, "trade", split_axis=0, concat_axis=0, tiled=True),
        lax.all_to_all(labels, "trade", split_axis=0, concat_axis=0, tiled=True),
    )
    received_rows = trade_values(arrived.reshape(-1, coefficients.shape[1]), path_basis)
    cva_held, shares = owner_shares(
        received_rows, arrived_labels, set_factor, set_level, default_date, discount
    )
    returned = lax.all_to_all(
        shares.reshape(owners, -1), "trade", split_axis=0, concat_axis=0, tiled=True
    )
    alloc_part = returned.reshape(-1)[target_row]
    alloc, set_cva = in_one((alloc_part, cva_held), "path")
    return (alloc, set_cva)


def solution(mesh):
    in_specs = (
        P("trade", None),
        P(None, "path"),
        P("trade", None),
        P("trade"),
        P("trade"),
        P("trade"),
        P(None, "path"),
        P(),
    )
    out_specs = (P("trade"), P("trade"))
    return jax.shard_map(
        on_device, mesh=mesh, in_specs=in_specs, out_specs=out_specs, check_vma=False
    )
```

profile of v0, /device:TPU:1, one launch (start us, length us, event | category | flops | bytes accessed | tf_op | source)
XLA Modules:
  0.0 122.7 jit_solution(13527935231376520709)
XLA Ops:
  0.6 0.0 copy-start.2
  0.6 0.0 copy-start.4
  0.7 0.0 copy-start.3
  0.7 0.0 copy-start
  0.7 0.8 fusion.37
  1.5 4.5 %reduce-window.6 = s32[16,16,128]{2,1,0:T(8,128)S(1)} reduce-window(s32[16,16,128]{2,1,0:T(8,128)S(1)} %fusion.37, s32[]{:T(128)} %constant.35.clone.1), window={size=1x1x128 pad=0_0x0_0x127_0}, to_apply=%region_0.0 | reduce-window | flops 4161536 | bytes 262148 | tf_op jit(solution)/shard_map/reduce-window
  6.0 0.4 slice_reduce_fusion
  6.5 0.2 reduce-window.9
  6.6 0.1 broadcast_add_fusion
  6.7 0.8 fusion.36
  7.5 0.7 compare_select_fusion.4
  8.2 0.7 convert_element_type.64
  8.9 14.6 %scatter_custom_fusion = bf16[3072]{0:T(1024)(128)(2,1)S(1)} fusion(s32[2048]{0:T(1024)S(1)} %bitcast.32, bf16[2048]{0:T(1024)(128)(2,1)S(1)} %convert_element_type.64, bf16[]{:T(256)} %constant.17.clone.1), kind=kCustom, calls=%fused_computation.94 | custom fusion | bytes 6146 | tf_op jit(solution)/shard_map/scatter | solution.py:73
  23.5 0.7 all_to_all.22
  24.2 8.4 %all-to-all-start = ((bf16[16,1,192]{2,1,0:T(2,128)(2,1)}), bf16[16,1,192]{2,1,0:T(2,128)(2,1)S(1)}, u32[]{:S(2)}, u32[]{:S(2)}) async-start(bf16[16,1,192]{2,1,0:T(2,128)(2,1)} %all_to_all.22), calls=%async_computation | async-start | bytes 32768 | tf_op jit(solution)/shard_map/all_to_all | solution.py:114
  32.6 11.0 %scatter_custom_fusion.1 = bf16[3072,256]{1,0:T(8,128)(2,1)} fusion(s32[2048]{0:T(1024)S(1)} %bitcast.33, bf16[2048,256]{1,0:T(8,128)(2,1)} %param.8, bf16[]{:T(256)} %constant.40.clone.1), kind=kCustom, calls=%fused_computation.31 | custom fusion | bytes 1573376 | tf_op jit(solution)/shard_map/scatter | solution.py:69
  43.6 0.0 all-to-all-done
  43.6 7.0 %all-to-all-start.1 = ((bf16[16,192,256]{2,1,0:T(8,128)(2,1)}), bf16[16,192,256]{2,1,0:T(8,128)(2,1)S(1)}, u32[]{:S(2)}, u32[]{:S(2)}) async-start(bf16[16,192,256]{2,1,0:T(8,128)(2,1)} %bitcast.28), calls=%async_computation.1 | async-start | bytes 3145728 | tf_op jit(solution)/shard_map/all_to_all | solution.py:113
  50.6 0.0 copy-done.2
  50.6 0.6 fusion.65
  53.7 0.0 copy-done.4
  53.8 0.0 copy-done.3
  53.8 0.0 copy-done
  53.8 0.3 convolution_multiply_fusion
  54.1 0.3 convolution_multiply_fusion.1
  54.4 0.3 convolution_multiply_fusion.3
  54.7 0.1 convert_reduce_fusion
  54.8 0.1 reshape.117
  54.8 16.7 %all-to-all-done.1 = bf16[16,192,256]{2,1,0:T(8,128)(2,1)S(1)} async-done(((bf16[16,192,256]{2,1,0:T(8,128)(2,1)}), bf16[16,192,256]{2,1,0:T(8,128)(2,1)S(1)}, u32[]{:S(2)}, u32[]{:S(2)}) %all-to-all-start.1) | async-done | bytes 1572896 | tf_op jit(solution)/shard_map/all_to_all | solution.py:113
  71.6 1.1 convolution_convert_fusion
  72.6 1.0 convolution_convert_fusion.1
  73.7 1.1 convolution_convert_fusion.2
  74.7 1.0 convolution_convert_fusion.3
  75.8 3.9 %fusion = f32[64,2048]{1,0:T(8,128)S(1)} fusion(bf16[3072,512]{0,1:T(8,128)(2,1)S(1)} %convolution_convert_fusion, bf16[3072,512]{0,1:T(8,128)(2,1)S(1)} %convolution_convert_fusion.1, bf16[3072,512]{0,1:T(8,128)(2,1)S(1)} %convolution_convert_fusion.2, bf16[3072,512]{0,1:T(8,128)(2,1)S(1)} %convolution_convert_fusion.3, f32[3072]{0:T(1024)S(1)} %reshape.117), kind=kOutput, calls=%fused_computation.3 | convolution fusion | flops 855834624 | bytes 13119488 | tf_op jit(solution)/shard_map/dot_general | solution.py:89
  79.7 1.1 multiply_reduce_fusion.3
  80.8 1.1 multiply_reduce_fusion.1
  82.0 1.1 multiply_reduce_fusion
  83.1 0.6 fusion.30
  83.7 1.1 multiply_reduce_fusion.2
  84.9 0.7 add.100
  85.6 6.2 %all-to-all-start.2 = ((f32[16,1,192]{2,1,0:T(1,128)}), f32[16,1,192]{2,1,0:T(1,128)S(1)}, u32[]{:S(2)}, u32[]{:S(2)}) async-start(f32[16,1,192]{2,1,0:T(1,128)} %add.100), calls=%async_computation.2 | async-start | bytes 32768 | tf_op jit(solution)/shard_map/all_to_all | solution.py:120
  91.8 6.4 %all-to-all-done.2 = f32[16,1,192]{2,1,0:T(1,128)S(1)} async-done(((f32[16,1,192]{2,1,0:T(1,128)}), f32[16,1,192]{2,1,0:T(1,128)S(1)}, u32[]{:S(2)}, u32[]{:S(2)}) %all-to-all-start.2) | async-done | bytes 12320 | tf_op jit(solution)/shard_map/all_to_all | solution.py:120
  98.2 0.1 reshape.116
  98.3 11.8 %gather_fusion = f32[2048]{0:T(1024)S(1)} fusion(f32[3072]{0:T(1024)S(1)} %reshape.116, s32[2048]{0:T(1024)S(1)} %broadcast_clamp_fusion), kind=kCustom, calls=%fused_computation | custom fusion | bytes 24576 | tf_op jit(solution)/shard_map/gather | solution.py:123
  110.2 11.4 %all_to_all.27 = f32[8,1,2112]{2,1,0:T(1,128)S(1)} all-to-all(f32[8,1,2112]{2,1,0:T(1,128)S(1)} %broadcast_in_dim.8), channel_id=1, replica_groups=mesh['trade'=16,'path'=8] {'path'}, dimensions={0} | all-to-all | bytes 135168 | tf_op jit(solution)/shard_map/all_to_all | solution.py:15
  121.5 0.1 reduce_sum.99
  121.6 0.6 slice.92
  122.2 0.5 slice.93
  (10 shorter events, 0.1 us)
Async XLA Ops:
  0.6 49.9 %copy-start.2 = (f32[4]{0:T(128)S(1)}, f32[4]{0:T(128)}, u32[]{:S(2)}) copy-start(f32[4]{0:T(128)} %param.15) | copy-start | bytes 52
  0.6 53.1 %copy-start.4 = (s32[64]{0:T(128)S(1)}, s32[64]{0:T(128)}, u32[]{:S(2)}) copy-start(s32[64]{0:T(128)} %param.13) | copy-start | bytes 772
  0.7 53.1 %copy-start.3 = (s32[64]{0:T(128)S(1)}, s32[64]{0:T(128)}, u32[]{:S(2)}) copy-start(s32[64]{0:T(128)} %param.12) | copy-start | bytes 772
  0.7 53.1 %copy-start = (s32[512,512]{1,0:T(8,128)S(1)}, s32[512,512]{1,0:T(8,128)}, u32[]{:S(2)}) copy-start(s32[512,512]{1,0:T(8,128)} %param.14) | copy-start | bytes 3145732
  24.2 19.4 %all-to-all-start = ((bf16[16,1,192]{2,1,0:T(2,128)(2,1)}), bf16[16,1,192]{2,1,0:T(2,128)(2,1)S(1)}, u32[]{:S(2)}, u32[]{:S(2)}) async-start(bf16[16,1,192]{2,1,0:T(2,128)(2,1)} %all_to_all.22), calls=%async_computation | async-start | bytes 32768 | tf_op jit(solution)/shard_map/all_to_all | solution.py:114
  43.6 28.0 %copy-start.1 = (bf16[256,512]{1,0:T(8,128)(2,1)S(1)}, bf16[256,512]{1,0:T(8,128)(2,1)}, u32[]{:S(2)}) copy-start(bf16[256,512]{1,0:T(8,128)(2,1)} %param.9) | copy-start | bytes 786436
  43.6 28.0 %all-to-all-start.1 = ((bf16[16,192,256]{2,1,0:T(8,128)(2,1)}), bf16[16,192,256]{2,1,0:T(8,128)(2,1)S(1)}, u32[]{:S(2)}, u32[]{:S(2)}) async-start(bf16[16,192,256]{2,1,0:T(8,128)(2,1)} %bitcast.28), calls=%async_computation.1 | async-start | bytes 3145728 | tf_op jit(solution)/shard_map/all_to_all | solution.py:113
  85.6 12.6 %all-to-all-start.2 = ((f32[16,1,192]{2,1,0:T(1,128)}), f32[16,1,192]{2,1,0:T(1,128)S(1)}, u32[]{:S(2)}, u32[]{:S(2)}) async-start(f32[16,1,192]{2,1,0:T(1,128)} %add.100), calls=%async_computation.2 | async-start | bytes 32768 | tf_op jit(solution)/shard_map/all_to_all | solution.py:120
where the time goes:
time: 123 us
  local copies, waits for them, and re-layouts  41 us (33%)
  waiting for transfers between devices  23.1 us (19%)
  starting transfers between devices  21.5 us (17%)
  matrix products  14.2 us (12%)
  blocking collectives  11.4 us (9%)
  other arithmetic  7.98 us (6%)
  between operations  3.42 us (3%)
    all_to_all x1, waiting for transfers between devices, on_device(): lax.all_to_all(packed, 'trade', split_axis=0, concat_axis=0, tiled=True)  16.7 us
    scatter x1, local copies, waits for them, and re-layouts, pack_rows(): labels = jnp.full((owners * capacity,), -1.0, jnp.bfloat16).at[target_row...  14.6 us
    gather x1, local copies, waits for them, and re-layouts, on_device(): alloc_part = returned.reshape(-1)[target_row]  11.8 us
    all_to_all x1, blocking collectives, copy_for_each(): return lax.all_to_all(copies, axis, split_axis=0, concat_axis=0, tiled=True)  11.4 us
    scatter x1, local copies, waits for them, and re-layouts, pack_rows(): jnp.zeros((owners * capacity, rows.shape[1]), jnp.bfloat16).at[target_row]  11 us
    all_to_all x1, starting transfers between devices, on_device(): lax.all_to_all(labels, 'trade', split_axis=0, concat_axis=0, tiled=True)  8.42 us
    all_to_all x1, starting transfers between devices, on_device(): lax.all_to_all(packed, 'trade', split_axis=0, concat_axis=0, tiled=True)  6.97 us
    all_to_all x1, waiting for transfers between devices, on_device(): lax.all_to_all(shares.reshape(owners, -1), 'trade', split_axis=0, concat_...  6.43 us
  transfers between devices with their start and end apart: 3, of which 2 were waited for; matrix products, arithmetic and copies ran while one was open for 10% of the time, Pallas kernels for 0%

commit v1 on v0

v1 whole, which is shorter than its diff:
```python
import jax
import jax.numpy as jnp
from jax import lax
from jax.experimental import pallas as pl
from jax.experimental.pallas import tpu as pltpu
from jax.sharding import PartitionSpec as P

MESH = pl.DeviceIdType.MESH
K = 64
DATES = 4
LANES = 128
level_step = 1.5


def grid_offsets(side):
    def far(step):
        return min(step, side - step)

    offsets = [(a, b) for a in range(side) for b in range(side) if a or b]
    return sorted(offsets, key=lambda o: -(far(o[0]) + far(o[1])))


def column_of(row, size):
    eye = lax.broadcasted_iota(jnp.int32, (size, size), 0) == lax.broadcasted_iota(
        jnp.int32, (size, size), 1
    )
    return jnp.sum(jnp.where(eye, row, 0.0), axis=1, keepdims=True)


def row_of(column, size):
    eye = lax.broadcasted_iota(jnp.int32, (size, size), 0) == lax.broadcasted_iota(
        jnp.int32, (size, size), 1
    )
    return jnp.sum(jnp.where(eye, column, 0.0), axis=0, keepdims=True)


def make_kernel(n_trade, n_path, side, n_set, trades, per_path, factors):
    half = n_set // 2
    rows = n_trade * half
    width = DATES * K
    offsets = grid_offsets(side)
    path_steps = sorted(range(1, n_path), key=lambda k: -min(k, n_path - k))

    def kernel(
        coef_hbm, basis_hbm, owner_hbm, slot_hbm, factor_hbm, level_hbm, date_hbm, disc_hbm,
        alloc_ref, cva_ref,
        coef, basis, owner, slot, factor, level, date, disc,
        onehot, part, arrived, net, gpart, gother, gall, cva_mine, cva_in, al_mine, al_in,
        in_sem, s1, r1, sd, rd, s3, r3, sc, rc, sa, ra,
    ):
        me = lax.axis_index("trade")
        lane = lax.axis_index("path")
        core = lax.rem(lane, 2)
        partner = lane + 1 - 2 * core
        me_a, me_b = me // side, lax.rem(me, side)
        others = [
            lax.rem(me_a + a, side) * side + lax.rem(me_b + b, side) for a, b in offsets
        ]
        on_path = [lax.rem(lane + k, n_path) for k in path_steps]

        loads = [
            pltpu.make_async_copy(src, dst, in_sem.at[i])
            for i, (src, dst) in enumerate(
                (
                    (owner_hbm, owner), (slot_hbm, slot), (coef_hbm, coef), (basis_hbm, basis),
                    (factor_hbm, factor), (level_hbm, level), (disc_hbm, disc), (date_hbm, date),
                )
            )
        ]
        for load in loads:
            load.start()

        barrier = pltpu.get_barrier_semaphore()
        for o in others:
            pl.semaphore_signal(barrier, inc=1, device_id={"trade": o}, device_id_type=MESH)
        for q in on_path:
            pl.semaphore_signal(barrier, inc=1, device_id={"path": q}, device_id_type=MESH)

        loads[0].wait()
        loads[1].wait()
        loc = slot[...] - half * core
        ids = jnp.where((loc >= 0) & (loc < half), owner[...] * half + loc, -1)
        which = lax.broadcasted_iota(jnp.int32, (rows, LANES), 0)
        for r in range(trades // LANES):
            hit = which == ids[r : r + 1, :]
            onehot[:, r * LANES : (r + 1) * LANES] = jnp.where(hit, 1.0, 0.0).astype(jnp.bfloat16)
        loads[2].wait()
        sums = jnp.dot(onehot[...], coef[...], preferred_element_type=jnp.float32)
        part[...] = sums.astype(jnp.bfloat16).reshape(n_trade, half, width)

        pl.semaphore_wait(barrier, len(others) + len(on_path))
        sends = []
        firsts = []
        for j, o in enumerate(others):
            copy = pltpu.make_async_remote_copy(
                src_ref=part.at[o], dst_ref=arrived.at[j], send_sem=s1.at[j], recv_sem=r1.at[j],
                device_id={"trade": o}, device_id_type=MESH,
            )
            copy.start()
            firsts.append(copy)

        loads[4].wait()
        loads[5].wait()
        loads[6].wait()
        limit = level_step * column_of(level[...].astype(jnp.float32), n_set)
        wanted = column_of(factor[...].astype(jnp.float32), n_set)
        pick = (
            lax.broadcasted_iota(jnp.int32, (n_set, factors), 1).astype(jnp.float32) == wanted
        )
        pick = jnp.where(pick, 1.0, 0.0).astype(jnp.bfloat16)
        loads[7].wait()
        dated = jnp.dot(
            pick, date[...].astype(jnp.float32).astype(jnp.bfloat16),
            preferred_element_type=jnp.float32,
        )
        loads[3].wait()

        total = part[me].astype(jnp.float32)
        for j, copy in enumerate(firsts):
            copy.wait_recv()
            total = total + arrived[j].astype(jnp.float32)
        net[core] = total
        swap = pltpu.make_async_remote_copy(
            src_ref=net.at[core], dst_ref=net.at[core], send_sem=sd.at[0], recv_sem=rd.at[0],
            device_id={"path": partner}, device_id_type=MESH,
        )
        swap.start()
        swap.wait_recv()
        sends.append(swap)

        both = net[...].reshape(n_set, width)
        high = both.astype(jnp.bfloat16)
        low = (both - high.astype(jnp.float32)).astype(jnp.bfloat16)
        moment_of = lax.broadcasted_iota(jnp.int32, (n_set, width), 1) // K
        zero = jnp.zeros_like(high)
        b = basis[...]
        stack_high = jnp.concatenate([jnp.where(moment_of == d, high, zero) for d in range(DATES)])
        stack_low = jnp.concatenate([jnp.where(moment_of == d, low, zero) for d in range(DATES)])
        netted = jnp.dot(stack_high, b, preferred_element_type=jnp.float32) + jnp.dot(
            stack_low, b, preferred_element_type=jnp.float32
        )
        cva = jnp.zeros((n_set, 1), jnp.float32)
        slopes = []
        for d in range(DATES):
            x = netted[d * n_set : (d + 1) * n_set] - limit
            e = jnp.exp(-jnp.abs(x))
            inv = 1.0 / (1.0 + e)
            plus = jnp.maximum(x, 0.0) + jnp.log1p(e)
            sig = jnp.where(x >= 0, inv, e * inv)
            factor_d = disc[0:1, d : d + 1] / (per_path * n_path)
            weight = jnp.where(dated == float(d), factor_d, 0.0)
            cva = cva + jnp.sum(weight * plus, axis=1, keepdims=True)
            slopes.append((weight * sig).astype(jnp.bfloat16))
        grads = lax.dot_general(
            jnp.concatenate(slopes), b, (((1,), (1,)), ((), ())),
            preferred_element_type=jnp.float32,
        )
        grad = jnp.zeros((n_set, width), jnp.float32)
        for d in range(DATES):
            grad = grad + jnp.where(moment_of == d, grads[d * n_set : (d + 1) * n_set], 0.0)
        gpart[...] = grad.reshape(2, half, width)
        swap = pltpu.make_async_remote_copy(
            src_ref=gpart.at[1 - core], dst_ref=gother, send_sem=sd.at[1], recv_sem=rd.at[1],
            device_id={"path": partner}, device_id_type=MESH,
        )
        swap.start()
        sends.append(swap)
        cva_mine[...] = row_of(cva, n_set)
        cvas = []
        for j, q in enumerate(on_path):
            copy = pltpu.make_async_remote_copy(
                src_ref=cva_mine, dst_ref=cva_in.at[j], send_sem=sc.at[j], recv_sem=rc.at[j],
                device_id={"path": q}, device_id_type=MESH,
            )
            cvas.append(copy)
        swap.wait_recv()
        gall[me] = (gpart[core] + gother[...]).astype(jnp.bfloat16)
        seconds = []
        for j, o in enumerate(others):
            copy = pltpu.make_async_remote_copy(
                src_ref=gall.at[me], dst_ref=gall.at[me], send_sem=s3.at[j], recv_sem=r3.at[j],
                device_id={"trade": o}, device_id_type=MESH,
            )
            copy.start()
            seconds.append(copy)
        for copy in cvas:
            copy.start()
        for copy in seconds:
            copy.wait_recv()

        g = gall[...].reshape(rows, width)
        block = 2 * LANES
        for r in range(trades // block):
            dots = lax.dot_general(
                g, coef[r * block : (r + 1) * block, :], (((1,), (1,)), ((), ())),
                preferred_element_type=jnp.float32,
            )
            for h in range(2):
                at = 2 * r + h
                hit = which == ids[at : at + 1, :]
                al_mine[at : at + 1, :] = jnp.sum(
                    jnp.where(hit, dots[:, h * LANES : (h + 1) * LANES], 0.0),
                    axis=0, keepdims=True,
                )
        lasts = []
        for j, q in enumerate(on_path):
            copy = pltpu.make_async_remote_copy(
                src_ref=al_mine, dst_ref=al_in.at[j], send_sem=sa.at[j], recv_sem=ra.at[j],
                device_id={"path": q}, device_id_type=MESH,
            )
            copy.start()
            lasts.append(copy)
        cva_total = cva_mine[...]
        for j, copy in enumerate(cvas):
            copy.wait_recv()
            cva_total = cva_total + cva_in[j]
        cva_ref[...] = cva_total
        for copy in firsts + sends + seconds + cvas:
            copy.wait_send()
        total_alloc = al_mine[...]
        for j, copy in enumerate(lasts):
            copy.wait_recv()
            total_alloc = total_alloc + al_in[j]
        alloc_ref[...] = total_alloc
        for copy in lasts:
            copy.wait_send()

    return kernel


def solution(mesh):
    n_trade, n_path = mesh.shape["trade"], mesh.shape["path"]
    side = 4

    def on_device(
        coefficients, path_basis, trade_owner, trade_slot, set_factor, set_level, default_date,
        discount,
    ):
        trades, width = coefficients.shape
        n_set = set_factor.shape[0]
        factors, per_path = default_date.shape
        half = n_set // 2
        tall = trades // LANES
        bf16, f32, i32 = jnp.bfloat16, jnp.float32, jnp.int32
        dma = pltpu.SemaphoreType.DMA
        alloc, cva = pl.pallas_call(
            make_kernel(n_trade, n_path, side, n_set, trades, per_path, factors),
            out_shape=(
                jax.ShapeDtypeStruct((tall, LANES), f32),
                jax.ShapeDtypeStruct((1, n_set), f32),
            ),
            in_specs=[pl.BlockSpec(memory_space=pl.ANY)] * 8,
            out_specs=(
                pl.BlockSpec(memory_space=pltpu.VMEM),
                pl.BlockSpec(memory_space=pltpu.VMEM),
            ),
            scratch_shapes=[
                pltpu.VMEM((trades, width), bf16),
                pltpu.VMEM((width, per_path), bf16),
                pltpu.VMEM((tall, LANES), i32),
                pltpu.VMEM((tall, LANES), i32),
                pltpu.VMEM((1, n_set), i32),
                pltpu.VMEM((1, n_set), i32),
                pltpu.VMEM((factors, per_path), i32),
                pltpu.VMEM((1, DATES), f32),
                pltpu.VMEM((n_trade * half, trades), bf16),
                pltpu.VMEM((n_trade, half, width), bf16),
                pltpu.VMEM((n_trade - 1, half, width), bf16),
                pltpu.VMEM((2, half, width), f32),
                pltpu.VMEM((2, half, width), f32),
                pltpu.VMEM((half, width), f32),
                pltpu.VMEM((n_trade, half, width), bf16),
                pltpu.VMEM((1, n_set), f32),
                pltpu.VMEM((n_path - 1, 1, n_set), f32),
                pltpu.VMEM((tall, LANES), f32),
                pltpu.VMEM((n_path - 1, tall, LANES), f32),
                dma((8,)),
                dma((n_trade - 1,)),
                dma((n_trade - 1,)),
                dma((2,)),
                dma((2,)),
                dma((n_trade - 1,)),
                dma((n_trade - 1,)),
                dma((n_path - 1,)),
                dma((n_path - 1,)),
                dma((n_path - 1,)),
                dma((n_path - 1,)),
            ],
            compiler_params=pltpu.CompilerParams(collective_id=0, has_side_effects=True),
        )(
            coefficients,
            path_basis,
            trade_owner.reshape(tall, LANES),
            trade_slot.reshape(tall, LANES),
            set_factor.reshape(1, n_set),
            set_level.reshape(1, n_set),
            default_date,
            discount.reshape(1, DATES),
        )
        return alloc.reshape(trades), cva.reshape(n_set)

    return jax.shard_map(
        on_device,
        mesh=mesh,
        in_specs=(
            P("trade", None),
            P(None, "path"),
            P("trade", None),
            P("trade"),
            P("trade"),
            P("trade"),
            P(None, "path"),
            P(),
        ),
        out_specs=(P("trade"), P("trade")),
        check_vma=False,
    )
```

time: 123 us -> 31.3 us (0.25)
  local copies, waits for them, and re-layouts: 41 us -> 1.81 us
  Pallas kernels: 0 us -> 28.7 us
  waiting for transfers between devices: 23.1 us -> 0 us
  starting transfers between devices: 21.5 us -> 0 us
  matrix products: 14.2 us -> 0 us
  blocking collectives: 11.4 us -> 0 us
  other arithmetic: 7.98 us -> 0 us
  between operations: 3.42 us -> 0.65 us
    pallas_call x0 -> x1, Pallas kernels: none -> 28.7 us  [on_device(): pl.pallas_call(make_kernel(n_trade, n_path, side, n_set, trades, per_path...]
    scatter x2 -> x0, local copies, waits for them, and re-layouts: 25.5 us -> none  [the longest x1 14.6 us: pack_rows(): labels = jnp.full((owners * capacity,), -1.0, jnp.bfloat16).at[target_row...]
    all_to_all x3 -> x0, waiting for transfers between devices: 23.1 us -> none  [the longest x1 16.7 us: on_device(): lax.all_to_all(packed, 'trade', split_axis=0, concat_axis=0, tiled=True)]
    all_to_all x3 -> x0, starting transfers between devices: 21.5 us -> none  [the longest x1 8.42 us: on_device(): lax.all_to_all(labels, 'trade', split_axis=0, concat_axis=0, tiled=True)]
    dot_general x13 -> x0, matrix products: 14.2 us -> none  [the longest x4 4.56 us: owner_shares(): lax.dot_general(member, slopes[:, moment * per_path:(moment + 1) * per_pa...]
    gather x1 -> x0, local copies, waits for them, and re-layouts: 11.8 us -> none  [on_device(): alloc_part = returned.reshape(-1)[target_row]]
    all_to_all x1 -> x0, blocking collectives: 11.4 us -> none  [copy_for_each(): return lax.all_to_all(copies, axis, split_axis=0, concat_axis=0, tiled=True)]
    another operation x3 -> x0, other arithmetic: 4.82 us -> none
  transfers between devices with their start and end apart: 3 -> 0, of which waited for: 2 -> 0; matrix products, arithmetic and copies ran while one was open for 10% -> 0% of each run, Pallas kernels for 0% -> 0%
where the time goes in v1:
time: 31.3 us; the launch traced here: 31.1 us
  Pallas kernels  28.7 us (92%)
  local copies, waits for them, and re-layouts  1.81 us (6%)
  between operations  0.65 us (2%)
    pallas_call x1, Pallas kernels, on_device(): pl.pallas_call(make_kernel(n_trade, n_path, side, n_set, trades, per_path...  28.7 us
    unnamed x4, local copies, waits for them, and re-layouts  1.81 us

profile of v1, /device:TPU:1, one launch (start us, length us, event | category | flops | bytes accessed | tf_op | source)
XLA Modules:
  0.0 31.1 jit_solution(4163260732708950648)
XLA Ops:
  0.6 28.7 %shard_map.95 = (f32[16,128]{1,0:T(8,128)}, f32[1,64]{1,0:T(1,128)}) custom-call(bf16[2048,256]{1,0:T(8,128)(2,1)} %coef_hbm.1, bf16[256,512]{1,0:T(8,128)(2,1)} %basis_hbm.1, s32[16,128]{1,0:T(8,128)} %bitcast.7, s32[16,128]{1,0:T(8,128)} %bitcast.8, s32[1,64]{1,0:T(1,128)} %bitcast.10, s32[1,64]{1,0:T(1,128)} %bitcast.11, s32[512,512]{1,0:T(8,128)} %date_hbm.1, ...), custom_call_target="tpu_custom_call" | custom-call | tf_op jit(solution)/shard_map/pallas_call | solution.py:246
  29.3 0.0 copy-start
  29.3 1.3 %copy.12 = f32[2048]{0:T(1024)} copy(f32[2048]{0:T(1024)} %bitcast.9) | data formatting | bytes 16384
  30.6 0.0 copy-done
  30.6 0.5 %copy.13 = f32[64]{0:T(128)} copy(f32[64]{0:T(128)S(1)} %bitcast.13) | data formatting | bytes 512
Async XLA Ops:
  29.3 1.3 %copy-start = (f32[1,64]{1,0:T(1,128)S(1)}, f32[1,64]{1,0:T(1,128)}, u32[]{:S(2)}) copy-start(f32[1,64]{1,0:T(1,128)} %get-tuple-element.5) | copy-start | bytes 772

commit v2 on v1

v2 whole, which is shorter than its diff:
```python
import jax
import jax.numpy as jnp
from jax import lax
from jax.experimental import pallas as pl
from jax.experimental.pallas import tpu as pltpu
from jax.sharding import PartitionSpec as P

MESH = pl.DeviceIdType.MESH
K = 64
DATES = 4
LANES = 128
level_step = 1.5


def grid_offsets(side):
    def far(step):
        return min(step, side - step)

    offsets = [(a, b) for a in range(side) for b in range(side) if a or b]
    return sorted(offsets, key=lambda o: -(far(o[0]) + far(o[1])))


def diagonal(rows, columns, first):
    at = lax.broadcasted_iota(jnp.int32, (rows, columns), 0) + first
    return at == lax.broadcasted_iota(jnp.int32, (rows, columns), 1)


def make_kernel(n_trade, n_path, side, n_set, trades, per_path, factors):
    half = n_set // 2
    rows = n_trade * half
    width = DATES * K
    offsets = grid_offsets(side)
    path_steps = sorted(range(1, n_path), key=lambda k: -min(k, n_path - k))

    def kernel(
        coef_hbm, basis_hbm, owner_hbm, slot_hbm, factor_hbm, level_hbm, date_hbm, disc_hbm,
        alloc_ref, cva_ref,
        coef, basis, basis_other, owner, slot, factor, level, date, disc,
        onehot, part, arrived, dated, dated_other, gall, cva_mine, cva_in, al_mine, al_in,
        in_sem, s1, r1, sd, rd, s3, r3, sc, rc, sa, ra,
    ):
        me = lax.axis_index("trade")
        lane = lax.axis_index("path")
        core = lax.rem(lane, 2)
        partner = lane + 1 - 2 * core
        me_a, me_b = me // side, lax.rem(me, side)
        others = [
            lax.rem(me_a + a, side) * side + lax.rem(me_b + b, side) for a, b in offsets
        ]
        on_path = [lax.rem(lane + k, n_path) for k in path_steps]

        barrier = pltpu.get_barrier_semaphore()
        for o in others:
            pl.semaphore_signal(barrier, inc=1, device_id={"trade": o}, device_id_type=MESH)
        for q in on_path:
            pl.semaphore_signal(barrier, inc=1, device_id={"path": q}, device_id_type=MESH)
        loads = [
            pltpu.make_async_copy(src, dst, in_sem.at[i])
            for i, (src, dst) in enumerate(
                (
                    (owner_hbm, owner), (slot_hbm, slot), (coef_hbm, coef), (basis_hbm, basis),
                    (factor_hbm, factor), (level_hbm, level), (disc_hbm, disc), (date_hbm, date),
                )
            )
        ]
        for load in loads:
            load.start()

        loads[0].wait()
        loads[1].wait()
        loc = slot[...] - half * core
        ids = jnp.where((loc >= 0) & (loc < half), owner[...] * half + loc, -1)
        which = lax.broadcasted_iota(jnp.int32, (rows, LANES), 0)
        for r in range(trades // LANES):
            hit = which == ids[r : r + 1, :]
            onehot[:, r * LANES : (r + 1) * LANES] = jnp.where(hit, 1.0, 0.0).astype(jnp.bfloat16)
        loads[2].wait()
        sums = jnp.dot(onehot[...], coef[...], preferred_element_type=jnp.float32)
        part[...] = sums.astype(jnp.bfloat16).reshape(n_trade, half, width)

        loads[3].wait()
        pl.semaphore_wait(barrier, len(others) + len(on_path))
        firsts = []
        for j, o in enumerate(others):
            copy = pltpu.make_async_remote_copy(
                src_ref=part.at[o], dst_ref=arrived.at[j], send_sem=s1.at[j], recv_sem=r1.at[j],
                device_id={"trade": o}, device_id_type=MESH,
            )
            copy.start()
            firsts.append(copy)
        swap_basis = pltpu.make_async_remote_copy(
            src_ref=basis, dst_ref=basis_other, send_sem=sd.at[0], recv_sem=rd.at[0],
            device_id={"path": partner}, device_id_type=MESH,
        )
        swap_basis.start()

        loads[4].wait()
        loads[5].wait()
        loads[6].wait()
        limit = level_step * jnp.sum(
            jnp.where(diagonal(half, n_set, half * core), level[...].astype(jnp.float32), 0.0),
            axis=1, keepdims=True,
        )
        wanted = jnp.sum(
            jnp.where(diagonal(n_set, n_set, 0), factor[...].astype(jnp.float32), 0.0),
            axis=1, keepdims=True,
        )
        pick = (
            lax.broadcasted_iota(jnp.int32, (n_set, factors), 1).astype(jnp.float32) == wanted
        )
        pick = jnp.where(pick, 1.0, 0.0).astype(jnp.bfloat16)
        loads[7].wait()
        dated[...] = jnp.dot(
            pick, date[...].astype(jnp.float32).astype(jnp.bfloat16),
            preferred_element_type=jnp.float32,
        ).reshape(2, half, per_path)
        swap_dates = pltpu.make_async_remote_copy(
            src_ref=dated.at[1 - core], dst_ref=dated_other, send_sem=sd.at[1], recv_sem=rd.at[1],
            device_id={"path": partner}, device_id_type=MESH,
        )
        swap_dates.start()
        swap_basis.wait_recv()
        swap_dates.wait_recv()

        total = part[me].astype(jnp.float32)
        for j in reversed(range(len(firsts))):
            firsts[j].wait_recv()
            total = total + arrived[j].astype(jnp.float32)

        high = total.astype(jnp.bfloat16)
        low = (total - high.astype(jnp.float32)).astype(jnp.bfloat16)
        moment_of = lax.broadcasted_iota(jnp.int32, (half, width), 1) // K
        zero = jnp.zeros_like(high)
        stack_high = jnp.concatenate([jnp.where(moment_of == d, high, zero) for d in range(DATES)])
        stack_low = jnp.concatenate([jnp.where(moment_of == d, low, zero) for d in range(DATES)])
        cva = jnp.zeros((half, 1), jnp.float32)
        grads = 0.0
        for b_ref, when in ((basis, dated[core]), (basis_other, dated_other[...])):
            b = b_ref[...]
            netted = jnp.dot(stack_high, b, preferred_element_type=jnp.float32) + jnp.dot(
                stack_low, b, preferred_element_type=jnp.float32
            )
            slopes = []
            for d in range(DATES):
                x = netted[d * half : (d + 1) * half] - limit
                e = jnp.exp(-jnp.abs(x))
                inv = 1.0 / (1.0 + e)
                plus = jnp.maximum(x, 0.0) + jnp.log1p(e)
                sig = jnp.where(x >= 0, inv, e * inv)
                factor_d = disc[0:1, d : d + 1] / (per_path * n_path)
                weight = jnp.where(when == float(d), factor_d, 0.0)
                cva = cva + jnp.sum(weight * plus, axis=1, keepdims=True)
                slopes.append((weight * sig).astype(jnp.bfloat16))
            grads = grads + lax.dot_general(
                jnp.concatenate(slopes), b, (((1,), (1,)), ((), ())),
                preferred_element_type=jnp.float32,
            )
        grad = jnp.zeros((half, width), jnp.float32)
        for d in range(DATES):
            grad = grad + jnp.where(moment_of == d, grads[d * half : (d + 1) * half], 0.0)
        gall[me] = grad.astype(jnp.bfloat16)
        seconds = []
        for j, o in enumerate(others):
            copy = pltpu.make_async_remote_copy(
                src_ref=gall.at[me], dst_ref=gall.at[me], send_sem=s3.at[j], recv_sem=r3.at[j],
                device_id={"trade": o}, device_id_type=MESH,
            )
            copy.start()
            seconds.append(copy)
        cva_mine[...] = jnp.sum(
            jnp.where(diagonal(half, n_set, half * core), cva, 0.0), axis=0, keepdims=True
        )
        cvas = []
        for j, q in enumerate(on_path):
            copy = pltpu.make_async_remote_copy(
                src_ref=cva_mine, dst_ref=cva_in.at[j], send_sem=sc.at[j], recv_sem=rc.at[j],
                device_id={"path": q}, device_id_type=MESH,
            )
            copy.start()
            cvas.append(copy)
        for copy in reversed(seconds):
            copy.wait_recv()

        g = gall[...].reshape(rows, width)
        block = 2 * LANES
        for r in range(trades // block):
            dots = lax.dot_general(
                g, coef[r * block : (r + 1) * block, :], (((1,), (1,)), ((), ())),
                preferred_element_type=jnp.float32,
            )
            for h in range(2):
                at = 2 * r + h
                hit = which == ids[at : at + 1, :]
                al_mine[at : at + 1, :] = jnp.sum(
                    jnp.where(hit, dots[:, h * LANES : (h + 1) * LANES], 0.0),
                    axis=0, keepdims=True,
                )
        lasts = []
        for j, q in enumerate(on_path):
            copy = pltpu.make_async_remote_copy(
                src_ref=al_mine, dst_ref=al_in.at[j], send_sem=sa.at[j], recv_sem=ra.at[j],
                device_id={"path": q}, device_id_type=MESH,
            )
            copy.start()
            lasts.append(copy)
        cva_total = cva_mine[...]
        for j, copy in enumerate(cvas):
            copy.wait_recv()
            cva_total = cva_total + cva_in[j]
        cva_ref[...] = cva_total
        for copy in firsts + [swap_basis, swap_dates] + seconds + cvas:
            copy.wait_send()
        total_alloc = al_mine[...]
        for j in reversed(range(len(lasts))):
            lasts[j].wait_recv()
            total_alloc = total_alloc + al_in[j]
        alloc_ref[...] = total_alloc
        for copy in lasts:
            copy.wait_send()

    return kernel


def write_out(alloc, cva, alloc_out, cva_out, sem):
    copies = [
        pltpu.make_async_copy(src, dst, sem.at[i])
        for i, (src, dst) in enumerate(((alloc, alloc_out), (cva, cva_out)))
    ]
    for copy in copies:
        copy.start()
    for copy in copies:
        copy.wait()


def solution(mesh):
    n_trade, n_path = mesh.shape["trade"], mesh.shape["path"]
    side = 4

    def on_device(
        coefficients, path_basis, trade_owner, trade_slot, set_factor, set_level, default_date,
        discount,
    ):
        trades, width = coefficients.shape
        n_set = set_factor.shape[0]
        factors, per_path = default_date.shape
        half = n_set // 2
        tall = trades // LANES
        bf16, f32, i32 = jnp.bfloat16, jnp.float32, jnp.int32
        dma = pltpu.SemaphoreType.DMA
        alloc, cva = pl.pallas_call(
            make_kernel(n_trade, n_path, side, n_set, trades, per_path, factors),
            out_shape=(pltpu.VMEM((tall, LANES), f32), pltpu.VMEM((1, n_set), f32)),
            in_specs=[pl.BlockSpec(memory_space=pl.ANY)] * 8,
            out_specs=(
                pl.BlockSpec(memory_space=pltpu.VMEM),
                pl.BlockSpec(memory_space=pltpu.VMEM),
            ),
            scratch_shapes=[
                pltpu.VMEM((trades, width), bf16),
                pltpu.VMEM((width, per_path), bf16),
                pltpu.VMEM((width, per_path), bf16),
                pltpu.VMEM((tall, LANES), i32),
                pltpu.VMEM((tall, LANES), i32),
                pltpu.VMEM((1, n_set), i32),
                pltpu.VMEM((1, n_set), i32),
                pltpu.VMEM((factors, per_path), i32),
                pltpu.VMEM((1, DATES), f32),
                pltpu.VMEM((n_trade * half, trades), bf16),
                pltpu.VMEM((n_trade, half, width), bf16),
                pltpu.VMEM((n_trade - 1, half, width), bf16),
                pltpu.VMEM((2, half, per_path), f32),
                pltpu.VMEM((half, per_path), f32),
                pltpu.VMEM((n_trade, half, width), bf16),
                pltpu.VMEM((1, n_set), f32),
                pltpu.VMEM((n_path - 1, 1, n_set), f32),
                pltpu.VMEM((tall, LANES), f32),
                pltpu.VMEM((n_path - 1, tall, LANES), f32),
                dma((8,)),
                dma((n_trade - 1,)),
                dma((n_trade - 1,)),
                dma((2,)),
                dma((2,)),
                dma((n_trade - 1,)),
                dma((n_trade - 1,)),
                dma((n_path - 1,)),
                dma((n_path - 1,)),
                dma((n_path - 1,)),
                dma((n_path - 1,)),
            ],
            compiler_params=pltpu.CompilerParams(collective_id=0, has_side_effects=True),
        )(
            coefficients,
            path_basis,
            trade_owner.reshape(tall, LANES),
            trade_slot.reshape(tall, LANES),
            set_factor.reshape(1, n_set),
            set_level.reshape(1, n_set),
            default_date,
            discount.reshape(1, DATES),
        )
        alloc, cva = pl.pallas_call(
            write_out,
            out_shape=(
                jax.ShapeDtypeStruct((tall, LANES), f32),
                jax.ShapeDtypeStruct((1, n_set), f32),
            ),
            in_specs=[pl.BlockSpec(memory_space=pltpu.VMEM)] * 2,
            out_specs=(
                pl.BlockSpec(memory_space=pltpu.HBM),
                pl.BlockSpec(memory_space=pltpu.HBM),
            ),
            scratch_shapes=[dma((2,))],
            compiler_params=pltpu.CompilerParams(vmem_limit_bytes=1 << 20),
        )(alloc, cva)
        return alloc.reshape(trades), cva.reshape(n_set)

    return jax.shard_map(
        on_device,
        mesh=mesh,
        in_specs=(
            P("trade", None),
            P(None, "path"),
            P("trade", None),
            P("trade"),
            P("trade"),
            P("trade"),
            P(None, "path"),
            P(),
        ),
        out_specs=(P("trade"), P("trade")),
        check_vma=False,
    )
```

time: 31.3 us -> 27.4 us (0.88)
  Pallas kernels: 28.7 us -> 26.6 us
  local copies, waits for them, and re-layouts: 1.81 us -> 0 us
    pallas_call x1, Pallas kernels: 28.7 us -> 26 us  [on_device(): pl.pallas_call(make_kernel(n_trade, n_path, side, n_set, trades, per_path...]
    unnamed x4 -> x0, local copies, waits for them, and re-layouts: 1.81 us -> none
    pallas_call x0 -> x1, Pallas kernels: none -> 0.62 us  [on_device(): pl.pallas_call(write_out, out_shape=(jax.ShapeDtypeStruct((tall, LANES),...]
where the time goes in v2:
time: 27.4 us; the launch traced here: 27.3 us
  Pallas kernels  26.6 us (97%)
  between operations  0.64 us (2%)
    pallas_call x1, Pallas kernels, on_device(): pl.pallas_call(make_kernel(n_trade, n_path, side, n_set, trades, per_path...  26 us
    pallas_call x1, Pallas kernels, on_device(): pl.pallas_call(write_out, out_shape=(jax.ShapeDtypeStruct((tall, LANES),...  0.62 us

profile of v2, /device:TPU:1, one launch (start us, length us, event | category | flops | bytes accessed | tf_op | source)
XLA Modules:
  0.0 27.3 jit_solution(10813378216021404510)
XLA Ops:
  0.6 26.0 %shard_map.95 = (f32[16,128]{1,0:T(8,128)S(1)}, f32[1,64]{1,0:T(1,128)S(1)}) custom-call(bf16[2048,256]{1,0:T(8,128)(2,1)} %coef_hbm.1, bf16[256,512]{1,0:T(8,128)(2,1)} %basis_hbm.1, s32[16,128]{1,0:T(8,128)} %bitcast.7, s32[16,128]{1,0:T(8,128)} %bitcast.8, s32[1,64]{1,0:T(1,128)} %bitcast.9, s32[1,64]{1,0:T(1,128)} %bitcast.10, s32[512,512]{1,0:T(8,128)} %date_hbm.1, ...), custom_call_target="tpu_custom_call" | custom-call | tf_op jit(solution)/shard_map/pallas_call | solution.py:250
  26.6 0.6 %shard_map.96 = (f32[16,128]{1,0:T(8,128)}, f32[1,64]{1,0:T(1,128)}) custom-call(f32[16,128]{1,0:T(8,128)S(1)} %get-tuple-element.6.alloc, f32[1,64]{1,0:T(1,128)S(1)} %get-tuple-element.7.cva), custom_call_target="tpu_custom_call" | custom-call | tf_op jit(solution)/shard_map/pallas_call | solution.py:301
